TPU v7x, 8 devices: a whole 2x2x1 slice. The times are simulated.
8 devices in a mesh: dp: 1 (over z), tp: 8 (over x, y, core).
Axes of the slice: x: 2, y: 2, z: 1, core: 2. Of those that a mesh axis runs over, the one named last changes fastest.
Arguments:
- x: bfloat16 [128, 12288], P('dp')
- w_gate: bfloat16 [12288, 33792], P(None, 'tp')
- w_up: bfloat16 [12288, 33792], P(None, 'tp')
- w_down: bfloat16 [33792, 12288], P('tp')
Outputs:
- output: bfloat16 [128, 12288], P('dp')
All inputs are finite; a program needn't handle non-finite values.
Results may differ from a plain program's by a relative error of at most 0.016.
Values are sent between devices in bfloat16 or wider.
A program may use at most 2 GiB of HBM per device.

v0:
```python
import jax
import jax.numpy as jnp
from jax import lax
from jax.sharding import PartitionSpec as P


def solution(mesh):
    def step(x, w_gate, w_up, w_down):
        gate = jnp.dot(x, w_gate, preferred_element_type=jnp.float32)
        up = jnp.dot(x, w_up, preferred_element_type=jnp.float32)
        hidden = (jax.nn.silu(gate) * up).astype(jnp.bfloat16)
        term = jnp.dot(hidden, w_down, preferred_element_type=jnp.float32).astype(jnp.bfloat16)
        return lax.psum(term, "tp")

    return jax.shard_map(
        step,
        mesh=mesh,
        in_specs=(P("dp", None), P(None, "tp"), P(None, "tp"), P("tp", None)),
        out_specs=P("dp", None),
        check_vma=False,
    )
```

profile of v0, /device:TPU:0, one launch (start us, length us, event | category | flops | bytes accessed | tf_op | source)
XLA Modules:
  0.0 188.0 jit_solution(2883564985715624922)
XLA Ops:
  6.5 0.0 copy-start
  6.5 0.0 all-reduce.2.cloned.1.call-start
  6.5 1.9 %copy-done = bf16[128,12288]{1,0:T(8,128)(2,1)S(1)} copy-done((bf16[128,12288]{1,0:T(8,128)(2,1)S(1)}, bf16[128,12288]{1,0:T(8,128)(2,1)}, u32[]{:S(2)}) %copy-start) | copy-done | bytes 3145752
  8.4 35.8 %fusion.1 = f32[128,4224]{1,0:T(8,128)} fusion(bf16[128,12288]{1,0:T(8,128)(2,1)S(1)} %copy-done, bf16[12288,4224]{1,0:T(8,128)(2,1)} %param.5), kind=kOutput, calls=%fused_computation.3 | convolution fusion | flops 13287555072 | bytes 109117440 | tf_op jit(solution)/shard_map/dot_general | solution.py:9
  44.2 35.6 %fusion = bf16[128,4224]{1,0:T(8,128)(2,1)} fusion(bf16[128,12288]{1,0:T(8,128)(2,1)S(1)} %copy-done, bf16[12288,4224]{1,0:T(8,128)(2,1)} %param.6, f32[128,4224]{1,0:T(8,128)} %fusion.1), kind=kOutput, calls=%fused_computation.2 | convolution fusion | flops 13290799104 | bytes 110198784 | tf_op jit(solution)/shard_map/dot_general | solution.py:10
  79.9 36.4 %convolution_convert_fusion = bf16[128,12288]{1,0:T(8,128)(2,1)} fusion(bf16[128,4224]{1,0:T(8,128)(2,1)} %fusion, bf16[4224,12288]{1,0:T(8,128)(2,1)} %param.7), kind=kOutput, calls=%fused_computation | convolution fusion | flops 13289127936 | bytes 108036096 | tf_op jit(solution)/shard_map/dot_general | solution.py:12
  116.3 0.0 all-reduce.2.cloned.1.call-update
  116.3 61.0 %all-reduce.2.cloned.1.call-done = bf16[128,12288]{1,0:T(8,128)(2,1)} async-done(((bf16[128,12288]{1,0:T(8,128)(2,1)}), bf16[128,12288]{1,0:T(8,128)(2,1)}) %all-reduce.2.cloned.1.call-update) | async-done | bytes 3145744 | tf_op jit(solution)/shard_map/psum | solution.py:13
  177.4 3.8 %copy.6 = bf16[128,12288]{1,0:T(8,128)(2,1)} copy(bf16[128,12288]{1,0:T(8,128)(2,1)} %all-reduce.2.cloned.1.call-done) | data formatting | bytes 6291456
Async XLA Ops:
  6.5 1.9 %copy-start = (bf16[128,12288]{1,0:T(8,128)(2,1)S(1)}, bf16[128,12288]{1,0:T(8,128)(2,1)}, u32[]{:S(2)}) copy-start(bf16[128,12288]{1,0:T(8,128)(2,1)} %param.4) | copy-start | bytes 9437188
  6.5 170.8 %all-reduce.2.cloned.1.call-start = ((), (), s32[]{:S(2)}) async-start(), calls=%async_computation | async-start | bytes 6291456 | tf_op jit(solution)/shard_map/psum | solution.py:13
Sparse Core Ops, SparseCore 0:
  116.4 60.8 all-reduce.1
where the time goes:
time: 188 us
  matrix products  108 us (57%)
  waiting for transfers between devices  61 us (32%)
  between operations  13.4 us (7%)
  local copies, waits for them, and re-layouts  5.72 us (3%)
    psum x1, waiting for transfers between devices, step(): return lax.psum(term, 'tp')  61 us
    dot_general x1, matrix products, step(): jnp.dot(hidden, w_down, preferred_element_type=jnp.float32)  36.4 us
    dot_general x1, matrix products, step(): gate = jnp.dot(x, w_gate, preferred_element_type=jnp.float32)  35.8 us
    dot_general x1, matrix products, step(): up = jnp.dot(x, w_up, preferred_element_type=jnp.float32)  35.6 us
    unnamed x3, local copies, waits for them, and re-layouts  5.72 us
  transfers between devices with their start and end apart: 1, of which 1 were waited for; matrix products, arithmetic and copies ran while one was open for 0% of the time, Pallas kernels for 0%

commit v1 on v0

v1 whole, which is shorter than its diff:
```python
import functools

import jax
import jax.numpy as jnp
from jax import lax
from jax.experimental import pallas as pl
from jax.experimental.pallas import tpu as pltpu
from jax.sharding import PartitionSpec as P

MESH = pl.DeviceIdType.MESH
ROWS, D, H = 128, 12288, 4224
KB = 1536
COLS = ((0, 1536), (1536, 1536), (3072, 1152))
NB = 512
CHUNKS = D // NB
SLOTS = 8
HALF = SLOTS // 2
LAGS = (1, 3, 5, 7, 9, 10)


def splits(width):
    return [(at, min(512, width - at)) for at in range(0, width, 512)]


def kernel(x_hbm, g_hbm, u_hbm, d_hbm, out_hbm, xv, hidden, acc_g, acc_u, ring, term, own, send0, recv0, send1, recv1,
           send2, recv2, y, x_sem, ring_sem, s0, r0, s1, r1, s2, r2, s3, r3, s4, r4, s5, r5, out_sem):
    me = lax.axis_index("tp")
    core = lax.rem(me, 2)
    cx, cy = me // 4, lax.rem(me // 2, 2)
    code = 4 * core + 2 * cx + cy
    partner = cx * 4 + cy * 2 + (1 - core)
    nbr_x = (1 - cx) * 4 + cy * 2 + core
    nbr_y = cx * 4 + (1 - cy) * 2 + core

    barrier = pltpu.get_barrier_semaphore()
    for peer in (partner, nbr_x, nbr_y):
        pl.semaphore_signal(barrier, inc=1, device_id={"tp": peer}, device_id_type=MESH)

    def x_copy(p):
        ccx, ccy, ccore = cx, cy, core
        if p & 1:
            ccy = 1 - ccy
        if p & 2:
            ccx = 1 - ccx
        if p & 4:
            ccore = 1 - ccore
        row = pl.multiple_of((4 * ccore + 2 * ccx + ccy) * 16, 16)
        return pltpu.make_async_copy(x_hbm.at[pl.ds(row, 16), :], xv.at[pl.ds(16 * p, 16), :], x_sem.at[p])

    def in_copy(w_hbm, nb, kb, slot):
        at, width = COLS[nb]
        return pltpu.make_async_copy(
            w_hbm.at[pl.ds(pl.multiple_of(kb * KB, KB), KB), pl.ds(at, width)],
            ring.at[slot, :, pl.ds(0, width)],
            ring_sem.at[slot, 0],
        )

    def down_copy(j, slot, r):
        at, depth = COLS[r]
        return pltpu.make_async_copy(
            d_hbm.at[pl.ds(at, depth), pl.ds(pl.multiple_of(j * NB, NB), NB)],
            ring.at[slot, pl.ds(0, depth), pl.ds(r * NB, NB)],
            ring_sem.at[slot, r],
        )

    for p in range(8):
        x_copy(p).start()
    for kb in range(HALF):
        in_copy(g_hbm, 0, kb, 2 * kb).start()
        in_copy(u_hbm, 0, kb, 2 * kb + 1).start()
    for p in range(8):
        x_copy(p).wait()

    for nb, (at, width) in enumerate(COLS):
        acc_g[...] = jnp.zeros_like(acc_g)
        acc_u[...] = jnp.zeros_like(acc_u)
        for late in (False, True):

            def body(t, _, nb=nb, width=width, late=late):
                kb = t + HALF if late else t
                xk = xv[:, pl.ds(pl.multiple_of(kb * KB, KB), KB)]
                for which, (w_hbm, acc) in enumerate(((g_hbm, acc_g), (u_hbm, acc_u))):
                    slot = 2 * t + which
                    in_copy(w_hbm, nb, kb, slot).wait()
                    for c, n in splits(width):
                        acc[:, c : c + n] += jnp.dot(xk, ring[slot, :, c : c + n], preferred_element_type=jnp.float32)
                    if not late:
                        in_copy(w_hbm, nb, kb + HALF, slot).start()
                    elif nb + 1 < len(COLS):
                        in_copy(w_hbm, nb + 1, t, slot).start()
                    else:
                        for r in range(3):
                            down_copy(slot, slot, r).start()
                return 0

            lax.fori_loop(0, HALF, body, 0)
        for c, n in splits(width):
            hidden[:, at + c : at + c + n] = (jax.nn.silu(acc_g[:, c : c + n]) * acc_u[:, c : c + n]).astype(jnp.bfloat16)

    pl.semaphore_wait(barrier, 3)

    def rdma(src, dst, send_sem, recv_sem, peer):
        return pltpu.make_async_remote_copy(
            src_ref=src, dst_ref=dst, send_sem=send_sem, recv_sem=recv_sem, device_id={"tp": peer}, device_id_type=MESH
        )

    def cols(c):
        return pl.ds(pl.multiple_of(c * NB, NB), NB)

    def c0(c):
        return rdma(send0.at[:, cols(c)], recv0.at[:, cols(c)], s0.at[c], r0.at[c], partner)

    def c1(c, odd):
        return rdma(send1.at[:, cols(c)], recv1.at[:, cols(c)], s1.at[c], r1.at[c], nbr_y if odd else nbr_x)

    def c2(c, odd):
        return rdma(send2.at[:, cols(c)], recv2.at[:, cols(c)], s2.at[c], r2.at[c], nbr_x if odd else nbr_y)

    def piece(core_, x_, y_):
        return pl.ds(pl.multiple_of((4 * core_ + 2 * x_ + y_) * 16, 16), 16)

    def c3(c, odd):
        at = y.at[piece(core, cx, cy), cols(c)]
        return rdma(at, at, s3.at[c], r3.at[c], nbr_x if odd else nbr_y)

    def c4(c, odd, second):
        if odd:
            at = y.at[piece(core, 1 - cx if second else cx, cy), cols(c)]
        else:
            at = y.at[piece(core, cx, 1 - cy if second else cy), cols(c)]
        return rdma(at, at, s4.at[c, int(second)], r4.at[c, int(second)], nbr_y if odd else nbr_x)

    def c5(c):
        at = y.at[pl.ds(pl.multiple_of(core * 64, 64), 64), cols(c)]
        return rdma(at, at, s5.at[c], r5.at[c], partner)

    def out_copy(c):
        return pltpu.make_async_copy(y.at[:, cols(c)], out_hbm.at[:, cols(c)], out_sem.at[c])

    def compute(c, odd, slot, more):
        for r in range(3):
            down_copy(c, slot, r).wait()
        total = None
        for r, (at, depth) in enumerate(COLS):
            part = jnp.dot(
                hidden[:, at : at + depth], ring[slot, :depth, r * NB : (r + 1) * NB], preferred_element_type=jnp.float32
            )
            total = part if total is None else total + part
        term[...] = total
        if more:
            for r in range(3):
                down_copy(c + SLOTS, slot, r).start()
        order = (0, 2, 1, 3) if odd else (0, 1, 2, 3)
        for q, p in enumerate(order):
            own[16 * q : 16 * q + 16, cols(c)] = term[16 * p : 16 * p + 16, :]
            send0[16 * q : 16 * q + 16, cols(c)] = term[64 + 16 * p : 80 + 16 * p, :].astype(jnp.bfloat16)
        c0(c).start()

    def stage1(c, odd):
        c0(c).wait_recv()
        total = own[:, cols(c)] + recv0[:, cols(c)].astype(jnp.float32)
        send1[:, cols(c)] = total[32:].astype(jnp.bfloat16)
        own[0:32, cols(c)] = total[:32]
        c1(c, odd).start()

    def stage2(c, odd):
        c1(c, odd).wait_recv()
        total = own[0:32, cols(c)] + recv1[:, cols(c)].astype(jnp.float32)
        send2[:, cols(c)] = total[16:].astype(jnp.bfloat16)
        own[0:16, cols(c)] = total[:16]
        c2(c, odd).start()

    def stage3(c, odd):
        c2(c, odd).wait_recv()
        total = own[0:16, cols(c)] + recv2[:, cols(c)].astype(jnp.float32)
        y[piece(core, cx, cy), cols(c)] = total.astype(jnp.bfloat16)
        c3(c, odd).start()
        c4(c, odd, False).start()

    def stage4(c, odd):
        c3(c, odd).wait_recv()
        c4(c, odd, True).start()

    def stage5(c, odd):
        c4(c, odd, False).wait_recv()
        c4(c, odd, True).wait_recv()
        c5(c).start()

    def stage6(c, odd):
        c5(c).wait_recv()
        out_copy(c).start()

    stages = tuple(zip(LAGS, (stage1, stage2, stage3, stage4, stage5, stage6)))

    def steps(lo, hi, computing, more):
        def pair(t, _):
            for odd in (0, 1):
                i = 2 * t + odd
                if computing:
                    compute(i, odd, lax.rem(i, SLOTS), more)
                for lag, stage in reversed(stages):
                    c = i - lag
                    c_odd = (odd + lag) % 2
                    if lo - lag >= 0 and hi - 1 - lag < CHUNKS:
                        stage(c, c_odd)
                    else:

                        @pl.when((c >= 0) & (c < CHUNKS))
                        def _(stage=stage, c=c, c_odd=c_odd):
                            stage(c, c_odd)

            return 0

        lax.fori_loop(lo // 2, hi // 2, pair, 0)

    steps(0, CHUNKS - SLOTS, True, True)
    steps(CHUNKS - SLOTS, CHUNKS, True, False)
    steps(CHUNKS, CHUNKS + LAGS[-1] + LAGS[-1] % 2, False, False)

    def drain(t, _):
        for odd in (0, 1):
            c = 2 * t + odd
            c0(c).wait_send()
            c1(c, odd).wait_send()
            c2(c, odd).wait_send()
            c3(c, odd).wait_send()
            c4(c, odd, False).wait_send()
            c4(c, odd, True).wait_send()
            c5(c).wait_send()
            out_copy(c).wait()
        return 0

    lax.fori_loop(0, CHUNKS // 2, drain, 0)


def solution(mesh):
    bf16, f32 = jnp.bfloat16, jnp.float32

    def step(x, w_gate, w_up, w_down):
        dma = pltpu.SemaphoreType.DMA
        return pl.pallas_call(
            kernel,
            out_shape=jax.ShapeDtypeStruct((ROWS, D), bf16),
            in_specs=[pl.BlockSpec(memory_space=pl.ANY)] * 4,
            out_specs=pl.BlockSpec(memory_space=pl.ANY),
            scratch_shapes=[
                pltpu.VMEM((ROWS, D), bf16),
                pltpu.VMEM((ROWS, H), bf16),
                pltpu.VMEM((ROWS, KB), f32),
                pltpu.VMEM((ROWS, KB), f32),
                pltpu.VMEM((SLOTS, KB, KB), bf16),
                pltpu.VMEM((ROWS, NB), f32),
                pltpu.VMEM((64, D), f32),
                pltpu.VMEM((64, D), bf16),
                pltpu.VMEM((64, D), bf16),
                pltpu.VMEM((32, D), bf16),
                pltpu.VMEM((32, D), bf16),
                pltpu.VMEM((16, D), bf16),
                pltpu.VMEM((16, D), bf16),
                pltpu.VMEM((ROWS, D), bf16),
                dma((8,)),
                dma((SLOTS, 3)),
                *[dma((CHUNKS,)) for _ in range(8)],
                dma((CHUNKS, 2)),
                dma((CHUNKS, 2)),
                dma((CHUNKS,)),
                dma((CHUNKS,)),
                dma((CHUNKS,)),
            ],
            compiler_params=pltpu.CompilerParams(
                collective_id=0, has_side_effects=True, vmem_limit_bytes=67_043_328
            ),
            cost_estimate=pl.CostEstimate(
                flops=6 * ROWS * D * H, bytes_accessed=6 * D * H + 4 * ROWS * D, transcendentals=ROWS * H
            ),
        )(x, w_gate, w_up, w_down)

    return jax.shard_map(
        step,
        mesh=mesh,
        in_specs=(P("dp", None), P(None, "tp"), P(None, "tp"), P("tp", None)),
        out_specs=P("dp", None),
        check_vma=False,
    )
```

time: 188 us -> 125 us (0.66)
  Pallas kernels: 0 us -> 121 us
  matrix products: 108 us -> 0 us
  waiting for transfers between devices: 61 us -> 0 us
  between operations: 13.4 us -> 0.01 us
  local copies, waits for them, and re-layouts: 5.72 us -> 3.83 us
    pallas_call x0 -> x1, Pallas kernels: none -> 121 us  [step(): pl.pallas_call(kernel, out_shape=jax.ShapeDtypeStruct((ROWS, D), bf16), i...]
    dot_general x3 -> x0, matrix products: 108 us -> none  [the longest x1 36.4 us: step(): jnp.dot(hidden, w_down, preferred_element_type=jnp.float32)]
    psum x1 -> x0, waiting for transfers between devices: 61 us -> none  [step(): return lax.psum(term, 'tp')]
    unnamed x3 -> x1, local copies, waits for them, and re-layouts: 5.72 us -> 3.83 us
  transfers between devices with their start and end apart: 1 -> 0, of which waited for: 1 -> 0; matrix products, arithmetic and copies ran while one was open for 0% -> 0% of each run, Pallas kernels for 0% -> 0%
where the time goes in v1:
time: 125 us
  Pallas kernels  121 us (97%)
  local copies, waits for them, and re-layouts  3.83 us (3%)
    pallas_call x1, Pallas kernels, step(): pl.pallas_call(kernel, out_shape=jax.ShapeDtypeStruct((ROWS, D), bf16), i...  121 us
    unnamed x1, local copies, waits for them, and re-layouts  3.83 us

profile of v1, /device:TPU:0, one launch (start us, length us, event | category | flops | bytes accessed | tf_op | source)
XLA Modules:
  0.0 125.2 jit_solution(10871799743893097202)
XLA Ops:
  0.0 121.4 %shard_map.46 = bf16[128,12288]{1,0:T(8,128)(2,1)} custom-call(bf16[128,12288]{1,0:T(8,128)(2,1)} %x_hbm.1, bf16[12288,4224]{1,0:T(8,128)(2,1)} %g_hbm.1, bf16[12288,4224]{1,0:T(8,128)(2,1)} %u_hbm.1, bf16[4224,12288]{1,0:T(8,128)(2,1)} %d_hbm.1), custom_call_target="tpu_custom_call" | custom-call | flops 39862665216 | bytes 317718528 | tf_op jit(solution)/shard_map/pallas_call | solution.py:241
  121.4 3.8 %copy.6 = bf16[128,12288]{1,0:T(8,128)(2,1)} copy(bf16[128,12288]{1,0:T(8,128)(2,1)} %shard_map.46) | data formatting | bytes 6291456

commit v2 on v1

--- a/solution.py
+++ b/solution.py
@@ -15,7 +15,7 @@
 CHUNKS = D // NB
 SLOTS = 8
 HALF = SLOTS // 2
-LAGS = (1, 3, 5, 7, 9, 10)
+LAGS = (2, 6, 10, 14, 18, 20)
 
 
 def splits(width):

time: 125 us -> 119 us (0.952)
  Pallas kernels: 121 us -> 115 us
    pallas_call x1, Pallas kernels: 121 us -> 115 us  [step(): pl.pallas_call(kernel, out_shape=jax.ShapeDtypeStruct((ROWS, D), bf16), i...]
where the time goes in v2:
time: 119 us; the launch traced here: 118 us
  Pallas kernels  115 us (97%)
  local copies, waits for them, and re-layouts  3.83 us (3%)
    pallas_call x1, Pallas kernels, step(): pl.pallas_call(kernel, out_shape=jax.ShapeDtypeStruct((ROWS, D), bf16), i...  115 us
    unnamed x1, local copies, waits for them, and re-layouts  3.83 us

profile of v2, /device:TPU:0, one launch (start us, length us, event | category | flops | bytes accessed | tf_op | source)
XLA Modules:
  0.0 118.5 jit_solution(728682708333254603)
XLA Ops:
  0.0 114.6 %shard_map.46 = bf16[128,12288]{1,0:T(8,128)(2,1)} custom-call(bf16[128,12288]{1,0:T(8,128)(2,1)} %x_hbm.1, bf16[12288,4224]{1,0:T(8,128)(2,1)} %g_hbm.1, bf16[12288,4224]{1,0:T(8,128)(2,1)} %u_hbm.1, bf16[4224,12288]{1,0:T(8,128)(2,1)} %d_hbm.1), custom_call_target="tpu_custom_call" | custom-call | flops 39862665216 | bytes 317718528 | tf_op jit(solution)/shard_map/pallas_call | solution.py:241
  114.6 3.8 %copy.6 = bf16[128,12288]{1,0:T(8,128)(2,1)} copy(bf16[128,12288]{1,0:T(8,128)(2,1)} %shard_map.46) | data formatting | bytes 6291456

commit v3 on v0

v3 whole, which is shorter than its diff:
```python
import jax
import jax.numpy as jnp
from jax import lax
from jax.experimental import pallas as pl
from jax.experimental.pallas import tpu as pltpu
from jax.sharding import PartitionSpec as P

MESH = pl.DeviceIdType.MESH
ROWS, D, H = 128, 12288, 4224
KB = 1536
COLS = ((0, 1536), (1536, 1536), (3072, 1152))
NB = 512
SLOTS = 8
HALF = SLOTS // 2

CHUNKS = [(512, "2", "2")] * 24
HOP, HOP2, D2D = 2.2, 3.2, 1.1
AXES = {1: ("y",), 2: ("x",), 3: ("x", "y")}


def plan():
    link, rate = 46.65e3, 3.44e6
    free = {"x": 0.0, "y": 0.0}
    arrive, t = [], 1.0
    for w, _, _ in CHUNKS:
        t += 2 * H * w / rate
        arrive.append(t)

    def send(axes, nbytes, now):
        end = max([now] + [free[a] for a in axes]) + nbytes / link
        for a in axes:
            free[a] = end
        return end + (HOP2 if len(axes) == 2 else HOP)

    def many(w, last, now):
        return max([now + D2D] + [send(AXES[p & 3], 32 * w, now) for p in range(1, last) if p & 3])

    order, pending, now, c_next = [], {}, 0.0, 0
    while c_next < len(CHUNKS) or pending:
        ripe = [c for c, v in pending.items() if v[1] <= now]
        if ripe:
            c = min(ripe)
        else:
            options = [(v[1], c) for c, v in pending.items()]
            if c_next < len(CHUNKS):
                options.append((max(arrive[c_next], now), c_next))
            c = min(options)[1]
        w, rs, ag = CHUNKS[c]
        far = AXES[2 if c % 2 == 0 else 1], AXES[1 if c % 2 == 0 else 2]
        if c == c_next:
            c_next += 1
            now = max(now, arrive[c]) + 0.65 * w / 512 + 0.05
            order.append((c, "compute"))
            pending[c] = ("all", many(w, 8, now)) if rs == "d" else ("pair", now + D2D + 128 * w / 650e3)
            continue
        event, at = pending.pop(c)
        now = max(now, at) + 0.08
        order.append((c, event))
        if event == "pair":
            pending[c] = ("first", send(far[0], 64 * w, now)) if rs == "2" else ("three", many(w, 4, now))
        elif event == "first":
            pending[c] = ("second", send(far[1], 32 * w, now))
        elif event in ("second", "three", "all"):
            if ag == "2":
                pending[c] = ("back", send(far[1], 32 * w, now))
                send(far[0], 32 * w, now)
            elif ag == "1":
                pending[c] = ("wide", many(w, 4, now))
            else:
                pending[c] = ("end", many(w, 8, now))
        elif event == "back":
            pending[c] = ("wide", send(far[0], 32 * w, now))
        elif event == "wide":
            pending[c] = ("end", now + D2D + 128 * w / 650e3)
    return order


def copies_of(rs, ag):
    return {"2": 3, "1": 4, "d": 7}[rs] + {"2": 4, "1": 4, "d": 7}[ag]


COPIES = sum(copies_of(rs, ag) for _, rs, ag in CHUNKS)
WIDE = max([w for w, rs, _ in CHUNKS if rs == "d"], default=0)


def blocks():
    out, at = [], 0
    for c, (w, _, _) in enumerate(CHUNKS):
        for b in range(0, w, NB):
            out.append((c, at + b, min(NB, w - b)))
        at += w
    return out


def splits(width):
    return [(at, min(512, width - at)) for at in range(0, width, 512)]


def kernel(x_hbm, g_hbm, u_hbm, d_hbm, y, xv, hidden, acc_g, acc_u, ring, term, own, send_a, recv_a, send_b, recv_b,
           send_d, recv_d, x_sem, ring_sem, send_sem, recv_sem):
    bf16, f32 = jnp.bfloat16, jnp.float32
    me = lax.axis_index("tp")
    place = lax.rem(me, 2), me // 4, lax.rem(me // 2, 2)

    def flip(p):
        return [1 - v if p >> b & 1 else v for v, b in zip(place, (2, 1, 0))]

    def device(p):
        core, x, y_ = flip(p)
        return 4 * x + 2 * y_ + core

    def piece(p):
        core, x, y_ = flip(p)
        return pl.ds(pl.multiple_of((4 * core + 2 * x + y_) * 16, 16), 16)

    barrier = pltpu.get_barrier_semaphore()
    for p in range(1, 8):
        pl.semaphore_signal(barrier, inc=1, device_id={"tp": device(p)}, device_id_type=MESH)

    def x_copy(p):
        return pltpu.make_async_copy(x_hbm.at[piece(p), :], xv.at[pl.ds(16 * p, 16), :], x_sem.at[p])

    def in_copy(w_hbm, nb, kb, slot):
        at, width = COLS[nb]
        return pltpu.make_async_copy(
            w_hbm.at[pl.ds(pl.multiple_of(kb * KB, KB), KB), pl.ds(at, width)],
            ring.at[slot, :, pl.ds(0, width)],
            ring_sem.at[slot, 0],
        )

    tiles = blocks()

    def down_copy(j, r):
        at, depth = COLS[r]
        _, col, w = tiles[j]
        return pltpu.make_async_copy(
            d_hbm.at[pl.ds(at, depth), pl.ds(col, w)],
            ring.at[j % SLOTS, pl.ds(0, depth), pl.ds(r * NB, w)],
            ring_sem.at[j % SLOTS, r],
        )

    for p in range(8):
        x_copy(p).start()
    for kb in range(HALF):
        in_copy(g_hbm, 0, kb, 2 * kb).start()
        in_copy(u_hbm, 0, kb, 2 * kb + 1).start()
    for p in range(8):
        x_copy(p).wait()

    for nb, (at, width) in enumerate(COLS):
        acc_g[...] = jnp.zeros_like(acc_g)
        acc_u[...] = jnp.zeros_like(acc_u)

        def multiply(kb, slot, nb=nb, width=width):
            xk = xv[:, pl.ds(pl.multiple_of(kb * KB, KB), KB)]
            w_hbm, acc = ((g_hbm, acc_g), (u_hbm, acc_u))[slot % 2 if isinstance(slot, int) else slot[1]]
            ref = slot if isinstance(slot, int) else slot[0]
            in_copy(w_hbm, nb, kb, ref).wait()
            for c, n in splits(width):
                acc[:, c : c + n] += jnp.dot(xk, ring[ref, :, c : c + n], preferred_element_type=f32)

        for late in (False, True):
            if late and nb + 1 == len(COLS):
                for t in range(HALF):
                    for which in range(2):
                        multiply(t + HALF, 2 * t + which)
                        for r in range(3):
                            down_copy(2 * t + which, r).start()
                continue

            def body(t, _, nb=nb, late=late):
                for which, w_hbm in enumerate((g_hbm, u_hbm)):
                    slot = 2 * t + which
                    multiply(t + HALF if late else t, (slot, which))
                    if late:
                        in_copy(w_hbm, nb + 1, t, slot).start()
                    else:
                        in_copy(w_hbm, nb, t + HALF, slot).start()
                return 0

            lax.fori_loop(0, HALF, body, 0)
        for c, n in splits(width):
            hidden[:, at + c : at + c + n] = (jax.nn.silu(acc_g[:, c : c + n]) * acc_u[:, c : c + n]).astype(bf16)

    pl.semaphore_wait(barrier, 7)

    started = []

    def send(src, dst, p):
        n = len(started)
        copy = pltpu.make_async_remote_copy(
            src_ref=src, dst_ref=dst, send_sem=send_sem.at[n], recv_sem=recv_sem.at[n],
            device_id={"tp": device(p)}, device_id_type=MESH,
        )
        copy.start()
        started.append(copy)
        return copy

    arriving = {}
    starts = [sum(w for w, _, _ in CHUNKS[:c]) for c in range(len(CHUNKS))]

    def compute(c, cols, axes):
        for j, (chunk, col, w) in enumerate(tiles):
            if chunk != c:
                continue
            total = None
            for r, (at, depth) in enumerate(COLS):
                down_copy(j, r).wait()
            for r, (at, depth) in enumerate(COLS):
                part = jnp.dot(
                    hidden[:, at : at + depth], ring[j % SLOTS, :depth, r * NB : r * NB + w], preferred_element_type=f32
                )
                total = part if total is None else total + part
            term[:, :w] = total
            if j + SLOTS < len(tiles):
                for r in range(3):
                    down_copy(j + SLOTS, r).start()
            here = slice(col, col + w)
            if CHUNKS[c][1] == "d":
                own[:16, here] = term[:16, :w]
                send_d[16:, :w] = term[16:, :w].astype(bf16)
                continue
            for q, p in enumerate((0, axes[1], axes[0], 3)):
                own[16 * q : 16 * q + 16, here] = term[16 * p : 16 * p + 16, :w]
                send_a[16 * q : 16 * q + 16, here] = term[64 + 16 * p : 80 + 16 * p, :w].astype(bf16)
        if CHUNKS[c][1] == "d":
            w = CHUNKS[c][0]
            arriving[c] = [
                send(send_d.at[16 * p : 16 * p + 16, :w], recv_d.at[16 * p : 16 * p + 16, :w], p) for p in (3, 7, 1, 2, 5, 6, 4)
            ]
        else:
            arriving[c] = [send(send_a.at[:, cols], recv_a.at[:, cols], 4)]

    def pair(c, cols, axes):
        total = own[:, cols] + recv_a[:, cols].astype(f32)
        if CHUNKS[c][1] == "2":
            send_b[:32, cols] = total[32:].astype(bf16)
            own[:32, cols] = total[:32]
            arriving[c] = [send(send_b.at[:32, cols], recv_b.at[:32, cols], axes[0])]
        else:
            send_b[:, cols] = total[16:].astype(bf16)
            own[:16, cols] = total[:16]
            arriving[c] = [
                send(send_b.at[16 * q - 16 : 16 * q, cols], recv_b.at[16 * q - 16 : 16 * q, cols], p)
                for q, p in ((3, 3), (1, axes[1]), (2, axes[0]))
            ]

    def first(c, cols, axes):
        total = own[:32, cols] + recv_b[:32, cols].astype(f32)
        send_b[32:, cols] = total[16:].astype(bf16)
        own[:16, cols] = total[:16]
        arriving[c] = [send(send_b.at[32:, cols], recv_b.at[32:, cols], axes[1])]

    def finish(c, cols, axes, total):
        y[piece(0), cols] = total.astype(bf16)
        at = y.at[piece(0), cols]
        ag = CHUNKS[c][2]
        if ag == "2":
            arriving[c] = [send(at, at, axes[1]), send(at, at, axes[0])]
        else:
            arriving[c] = [send(at, at, p) for p in ((3, 1, 2) if ag == "1" else (3, 7, 1, 2, 5, 6, 4))]

    def second(c, cols, axes):
        finish(c, cols, axes, own[:16, cols] + recv_b[32:, cols].astype(f32))

    def three(c, cols, axes):
        total = own[:16, cols]
        for q in range(3):
            total = total + recv_b[16 * q : 16 * q + 16, cols].astype(f32)
        finish(c, cols, axes, total)

    def all_(c, cols, axes):
        w = CHUNKS[c][0]
        total = own[:16, cols]
        for p in range(1, 8):
            total = total + recv_d[16 * p : 16 * p + 16, :w].astype(f32)
        finish(c, cols, axes, total)

    def back(c, cols, axes):
        at = y.at[piece(axes[1]), cols]
        arriving[c] = [arriving[c][1], send(at, at, axes[0])]

    def wide(c, cols, axes):
        at = y.at[pl.ds(pl.multiple_of(place[0] * 64, 64), 64), cols]
        arriving[c] = [send(at, at, 4)]

    events = {"pair": pair, "first": first, "second": second, "three": three, "all": all_, "back": back, "wide": wide}
    for c, event in plan():
        cols = slice(starts[c], starts[c] + CHUNKS[c][0])
        axes = (2, 1) if c % 2 == 0 else (1, 2)
        if event == "compute":
            compute(c, cols, axes)
            continue
        for copy in arriving[c][:1] if event == "back" else arriving[c]:
            copy.wait_recv()
        if event != "end":
            events[event](c, cols, axes)

    for copy in started:
        copy.wait_send()


def solution(mesh):
    bf16, f32 = jnp.bfloat16, jnp.float32

    def step(x, w_gate, w_up, w_down):
        dma = pltpu.SemaphoreType.DMA
        return pl.pallas_call(
            kernel,
            out_shape=pltpu.VMEM((ROWS, D), bf16),
            in_specs=[pl.BlockSpec(memory_space=pl.ANY)] * 4,
            out_specs=pl.BlockSpec(memory_space=pltpu.VMEM),
            scratch_shapes=[
                pltpu.VMEM((ROWS, D), bf16),
                pltpu.VMEM((ROWS, H), bf16),
                pltpu.VMEM((ROWS, KB), f32),
                pltpu.VMEM((ROWS, KB), f32),
                pltpu.VMEM((SLOTS, KB, KB), bf16),
                pltpu.VMEM((ROWS, NB), f32),
                pltpu.VMEM((64, D), f32),
                pltpu.VMEM((64, D), bf16),
                pltpu.VMEM((64, D), bf16),
                pltpu.VMEM((48, D), bf16),
                pltpu.VMEM((48, D), bf16),
                pltpu.VMEM((ROWS, max(WIDE, 128)), bf16),
                pltpu.VMEM((ROWS, max(WIDE, 128)), bf16),
                dma((8,)),
                dma((SLOTS, 3)),
                dma((COPIES,)),
                dma((COPIES,)),
            ],
            compiler_params=pltpu.CompilerParams(
                collective_id=0, has_side_effects=True, vmem_limit_bytes=60 << 20
            ),
            cost_estimate=pl.CostEstimate(
                flops=6 * ROWS * D * H, bytes_accessed=6 * D * H + 4 * ROWS * D, transcendentals=ROWS * H
            ),
        )(x, w_gate, w_up, w_down)

    return jax.shard_map(
        step,
        mesh=mesh,
        in_specs=(P("dp", None), P(None, "tp"), P(None, "tp"), P("tp", None)),
        out_specs=P("dp", None),
        check_vma=False,
    )
```

time: 188 us -> 115 us (0.61)
  Pallas kernels: 0 us -> 114 us
  matrix products: 108 us -> 0 us
  waiting for transfers between devices: 61 us -> 0 us
  between operations: 13.4 us -> 0.01 us
  local copies, waits for them, and re-layouts: 5.72 us -> 1.67 us
    pallas_call x0 -> x1, Pallas kernels: none -> 114 us  [step(): pl.pallas_call(kernel, out_shape=pltpu.VMEM((ROWS, D), bf16), in_specs=[p...]
    dot_general x3 -> x0, matrix products: 108 us -> none  [the longest x1 36.4 us: step(): jnp.dot(hidden, w_down, preferred_element_type=jnp.float32)]
    psum x1 -> x0, waiting for transfers between devices: 61 us -> none  [step(): return lax.psum(term, 'tp')]
    unnamed x3 -> x1, local copies, waits for them, and re-layouts: 5.72 us -> 1.67 us
  transfers between devices with their start and end apart: 1 -> 0, of which waited for: 1 -> 0; matrix products, arithmetic and copies ran while one was open for 0% -> 0% of each run, Pallas kernels for 0% -> 0%
where the time goes in v3:
time: 115 us
  Pallas kernels  114 us (99%)
  local copies, waits for them, and re-layouts  1.67 us (1%)
    pallas_call x1, Pallas kernels, step(): pl.pallas_call(kernel, out_shape=pltpu.VMEM((ROWS, D), bf16), in_specs=[p...  114 us

profile of v3, /device:TPU:0, one launch (start us, length us, event | category | flops | bytes accessed | tf_op | source)
XLA Modules:
  0.0 115.4 jit_solution(7022973829837286079)
XLA Ops:
  0.0 113.7 %shard_map.46 = bf16[128,12288]{1,0:T(8,128)(2,1)S(1)} custom-call(bf16[128,12288]{1,0:T(8,128)(2,1)} %x_hbm.1, bf16[12288,4224]{1,0:T(8,128)(2,1)} %g_hbm.1, bf16[12288,4224]{1,0:T(8,128)(2,1)} %u_hbm.1, bf16[4224,12288]{1,0:T(8,128)(2,1)} %d_hbm.1), custom_call_target="tpu_custom_call" | custom-call | flops 39862665216 | bytes 317718528 | tf_op jit(solution)/shard_map/pallas_call | solution.py:308
  113.7 1.7 %copy.6 = bf16[128,12288]{1,0:T(8,128)(2,1)} copy(bf16[128,12288]{1,0:T(8,128)(2,1)S(1)} %shard_map.46) | data formatting | bytes 6291456

commit v4 on v3

--- a/solution.py
+++ b/solution.py
@@ -13,8 +13,8 @@
 SLOTS = 8
 HALF = SLOTS // 2
 
-CHUNKS = [(512, "2", "2")] * 24
-HOP, HOP2, D2D = 2.2, 3.2, 1.1
+CHUNKS = [(512, "1", "1")] * 24
+HOP, HOP2, D2D = 3.0, 3.9, 1.4
 AXES = {1: ("y",), 2: ("x",), 3: ("x", "y")}
 
 

time: 115 us -> 114 us (level)
  Pallas kernels: 114 us -> 112 us
    pallas_call x1, Pallas kernels: 114 us -> 112 us  [step(): pl.pallas_call(kernel, out_shape=pltpu.VMEM((ROWS, D), bf16), in_specs=[p...]
where the time goes in v4:
time: 114 us
  Pallas kernels  112 us (98%)
  local copies, waits for them, and re-layouts  1.67 us (1%)
    pallas_call x1, Pallas kernels, step(): pl.pallas_call(kernel, out_shape=pltpu.VMEM((ROWS, D), bf16), in_specs=[p...  112 us

profile of v4, /device:TPU:0, one launch (start us, length us, event | category | flops | bytes accessed | tf_op | source)
XLA Modules:
  0.0 113.8 jit_solution(4277268882281418028)
XLA Ops:
  0.0 112.1 %shard_map.46 = bf16[128,12288]{1,0:T(8,128)(2,1)S(1)} custom-call(bf16[128,12288]{1,0:T(8,128)(2,1)} %x_hbm.1, bf16[12288,4224]{1,0:T(8,128)(2,1)} %g_hbm.1, bf16[12288,4224]{1,0:T(8,128)(2,1)} %u_hbm.1, bf16[4224,12288]{1,0:T(8,128)(2,1)} %d_hbm.1), custom_call_target="tpu_custom_call" | custom-call | flops 39862665216 | bytes 317718528 | tf_op jit(solution)/shard_map/pallas_call | solution.py:308
  112.1 1.7 %copy.6 = bf16[128,12288]{1,0:T(8,128)(2,1)} copy(bf16[128,12288]{1,0:T(8,128)(2,1)S(1)} %shard_map.46) | data formatting | bytes 6291456

commit v5 on v4

--- a/solution.py
+++ b/solution.py
@@ -13,13 +13,13 @@
 SLOTS = 8
 HALF = SLOTS // 2
 
-CHUNKS = [(512, "1", "1")] * 24
-HOP, HOP2, D2D = 3.0, 3.9, 1.4
+CHUNKS = [(512, "2", "2")] * 20 + [(512, "1", "2")] * 2 + [(512, "1", "1")] * 2
+HOP, HOP2, D2D = 2.7, 3.55, 1.6
 AXES = {1: ("y",), 2: ("x",), 3: ("x", "y")}
 
 
 def plan():
-    link, rate = 46.65e3, 3.44e6
+    link, rate = 41e3, 3.44e6
     free = {"x": 0.0, "y": 0.0}
     arrive, t = [], 1.0
     for w, _, _ in CHUNKS:
@@ -39,7 +39,7 @@
     while c_next < len(CHUNKS) or pending:
         ripe = [c for c, v in pending.items() if v[1] <= now]
         if ripe:
-            c = min(ripe)
+            c = max(ripe)
         else:
             options = [(v[1], c) for c, v in pending.items()]
             if c_next < len(CHUNKS):
@@ -49,7 +49,7 @@
         far = AXES[2 if c % 2 == 0 else 1], AXES[1 if c % 2 == 0 else 2]
         if c == c_next:
             c_next += 1
-            now = max(now, arrive[c]) + 0.65 * w / 512 + 0.05
+            now = max(now, arrive[c]) + 0.7 * w / 512 + 0.05
             order.append((c, "compute"))
             pending[c] = ("all", many(w, 8, now)) if rs == "d" else ("pair", now + D2D + 128 * w / 650e3)
             continue

time: 114 us -> 113 us (level)
  no operation moved by 1% of the time
where the time goes in v5:
time: 113 us
  Pallas kernels  112 us (99%)
  local copies, waits for them, and re-layouts  1.67 us (1%)
    pallas_call x1, Pallas kernels, step(): pl.pallas_call(kernel, out_shape=pltpu.VMEM((ROWS, D), bf16), in_specs=[p...  112 us

profile of v5, /device:TPU:0, one launch (start us, length us, event | category | flops | bytes accessed | tf_op | source)
XLA Modules:
  0.0 113.2 jit_solution(7059116468427631862)
XLA Ops:
  0.0 111.6 %shard_map.46 = bf16[128,12288]{1,0:T(8,128)(2,1)S(1)} custom-call(bf16[128,12288]{1,0:T(8,128)(2,1)} %x_hbm.1, bf16[12288,4224]{1,0:T(8,128)(2,1)} %g_hbm.1, bf16[12288,4224]{1,0:T(8,128)(2,1)} %u_hbm.1, bf16[4224,12288]{1,0:T(8,128)(2,1)} %d_hbm.1), custom_call_target="tpu_custom_call" | custom-call | flops 39862665216 | bytes 317718528 | tf_op jit(solution)/shard_map/pallas_call | solution.py:308
  111.6 1.7 %copy.6 = bf16[128,12288]{1,0:T(8,128)(2,1)} copy(bf16[128,12288]{1,0:T(8,128)(2,1)S(1)} %shard_map.46) | data formatting | bytes 6291456

commit v6 on v0

v6 whole, which is shorter than its diff:
```python
import jax
import jax.numpy as jnp
from jax import lax
from jax.experimental import pallas as pl
from jax.experimental.pallas import tpu as pltpu
from jax.sharding import PartitionSpec as P

MESH = pl.DeviceIdType.MESH
ROWS, D, H = 128, 12288, 4224
KB = 1536
COLS = ((0, 1536), (1536, 1536), (3072, 1152))
NB = 512
CHUNKS = D // NB
TWO = 20
LAGS_TWO = (1, 4, 7, 10, 13, 15)
LAGS_ONE = (1, 5, 9, 11)
SLOTS = 8
WIDTH = 1408
KS, TILES = D // KB, D // KB * (H // WIDTH)

def splits(width):
    return [(at, min(512, width - at)) for at in range(0, width, 512)]


def kernel(x_hbm, g_hbm, u_hbm, d_hbm, y, xv, hidden, acc_g, acc_u, ring, term, own, send_a, recv_a, send_b, recv_b,
           x_sem, ring_sem, send_sem, recv_sem):
    bf16, f32 = jnp.bfloat16, jnp.float32
    me = lax.axis_index("tp")
    place = lax.rem(me, 2), me // 4, lax.rem(me // 2, 2)

    def flip(p):
        return [1 - v if p >> b & 1 else v for v, b in zip(place, (2, 1, 0))]

    def device(p):
        core, x, y_ = flip(p)
        return 4 * x + 2 * y_ + core

    def piece(p):
        core, x, y_ = flip(p)
        return pl.ds(pl.multiple_of((4 * core + 2 * x + y_) * 16, 16), 16)

    barrier = pltpu.get_barrier_semaphore()
    for p in range(1, 8):
        pl.semaphore_signal(barrier, inc=1, device_id={"tp": device(p)}, device_id_type=MESH)

    def x_copy(p):
        return pltpu.make_async_copy(x_hbm.at[piece(p), :], xv.at[pl.ds(16 * p, 16), :], x_sem.at[p])

    def in_copy(w_hbm, t, slot):
        row = pl.multiple_of(lax.rem(t, KS) * KB, KB)
        col = pl.multiple_of(t // KS * WIDTH, 128)
        return pltpu.make_async_copy(
            w_hbm.at[pl.ds(row, KB), pl.ds(col, WIDTH)], ring.at[slot, :, pl.ds(0, WIDTH)], ring_sem.at[slot, 0]
        )

    def cols(c):
        return pl.ds(pl.multiple_of(c * NB, NB), NB)

    def down_copy(c, slot, r):
        at, depth = COLS[r]
        return pltpu.make_async_copy(
            d_hbm.at[pl.ds(at, depth), cols(c)], ring.at[slot, pl.ds(0, depth), pl.ds(r * NB, NB)], ring_sem.at[slot, r]
        )

    for p in range(8):
        x_copy(p).start()
    for t in range(SLOTS // 2):
        in_copy(g_hbm, t, 2 * t).start()
        in_copy(u_hbm, t, 2 * t + 1).start()
    for p in range(8):
        x_copy(p).wait()

    def project(t, _):
        kb = lax.rem(t, KS)

        @pl.when(kb == 0)
        def _():
            acc_g[...] = jnp.zeros_like(acc_g)
            acc_u[...] = jnp.zeros_like(acc_u)

        xk = xv[:, pl.ds(pl.multiple_of(kb * KB, KB), KB)]
        for which, (w_hbm, acc) in enumerate(((g_hbm, acc_g), (u_hbm, acc_u))):
            slot = 2 * lax.rem(t, SLOTS // 2) + which
            in_copy(w_hbm, t, slot).wait()
            for c, n in splits(WIDTH):
                acc[:, c : c + n] += jnp.dot(xk, ring[slot, :, c : c + n], preferred_element_type=f32)

            @pl.when(t < TILES - SLOTS // 2)
            def _(w_hbm=w_hbm, slot=slot):
                in_copy(w_hbm, t + SLOTS // 2, slot).start()

            @pl.when(t >= TILES - SLOTS // 2)
            def _(slot=slot):
                for r in range(3):
                    down_copy(slot, slot, r).start()

        @pl.when(kb == KS - 1)
        def _():
            for c, n in splits(WIDTH):
                at = pl.ds(pl.multiple_of(t // KS * WIDTH + c, 128), n)
                hidden[:, at] = (jax.nn.silu(acc_g[:, c : c + n]) * acc_u[:, c : c + n]).astype(bf16)

        return 0

    lax.fori_loop(0, TILES, project, 0)

    pl.semaphore_wait(barrier, 7)

    def copy(k, src, dst, c, p):
        return pltpu.make_async_remote_copy(
            src_ref=src, dst_ref=dst, send_sem=send_sem.at[k, c], recv_sem=recv_sem.at[k, c],
            device_id={"tp": device(p)}, device_id_type=MESH,
        )

    def axes_of(odd):
        return (1, 2) if odd else (2, 1)

    def pair_copy(c):
        return copy(0, send_a.at[:, cols(c)], recv_a.at[:, cols(c)], c, 4)

    def sum_copy(c, k, rows, p):
        return copy(k, send_b.at[rows, cols(c)], recv_b.at[rows, cols(c)], c, p)

    def first_copy(c, odd):
        return sum_copy(c, 1, pl.ds(0, 32), axes_of(odd)[0])

    def second_copy(c, odd):
        return sum_copy(c, 2, pl.ds(32, 16), axes_of(odd)[1])

    def three_copies(c, odd):
        a, b = axes_of(odd)
        return [sum_copy(c, k, pl.ds(16 * k - 16, 16), p) for k, p in ((3, 3), (1, b), (2, a))]

    def out_copy(c, k, owner, p):
        at = y.at[piece(owner), cols(c)]
        return copy(k, at, at, c, p)

    def two_copies(c, odd):
        a, b = axes_of(odd)
        return [out_copy(c, 4, 0, b), out_copy(c, 5, 0, a)]

    def back_copy(c, odd):
        a, b = axes_of(odd)
        return out_copy(c, 7, b, a)

    def all_copies(c):
        return [out_copy(c, 7, 0, 3), out_copy(c, 4, 0, 1), out_copy(c, 5, 0, 2)]

    def wide_copy(c):
        at = y.at[pl.ds(pl.multiple_of(place[0] * 64, 64), 64), cols(c)]
        return copy(6, at, at, c, 4)

    def compute(c, odd):
        slot = lax.rem(c, SLOTS)
        for r in range(3):
            down_copy(c, slot, r).wait()
        total = None
        for r, (at, depth) in enumerate(COLS):
            part = jnp.dot(
                hidden[:, at : at + depth], ring[slot, :depth, r * NB : (r + 1) * NB], preferred_element_type=f32
            )
            total = part if total is None else total + part
        term[...] = total

        @pl.when(c + SLOTS < CHUNKS)
        def _():
            for r in range(3):
                down_copy(c + SLOTS, slot, r).start()

        a, b = axes_of(odd)
        for q, p in enumerate((0, b, a, 3)):
            own[16 * q : 16 * q + 16, cols(c)] = term[16 * p : 16 * p + 16, :]
            send_a[16 * q : 16 * q + 16, cols(c)] = term[64 + 16 * p : 80 + 16 * p, :].astype(bf16)
        pair_copy(c).start()

    def start(copies):
        for one in copies:
            one.start()

    def pair_two(c, odd):
        pair_copy(c).wait_recv()
        total = own[:, cols(c)] + recv_a[:, cols(c)].astype(f32)
        send_b[:32, cols(c)] = total[32:].astype(bf16)
        own[:32, cols(c)] = total[:32]
        first_copy(c, odd).start()

    def first(c, odd):
        first_copy(c, odd).wait_recv()
        total = own[:32, cols(c)] + recv_b[:32, cols(c)].astype(f32)
        send_b[32:, cols(c)] = total[16:].astype(bf16)
        own[:16, cols(c)] = total[:16]
        second_copy(c, odd).start()

    def second(c, odd):
        second_copy(c, odd).wait_recv()
        y[piece(0), cols(c)] = (own[:16, cols(c)] + recv_b[32:, cols(c)].astype(f32)).astype(bf16)
        start(two_copies(c, odd))

    def back(c, odd):
        two_copies(c, odd)[0].wait_recv()
        back_copy(c, odd).start()

    def wide_two(c, odd):
        two_copies(c, odd)[1].wait_recv()
        back_copy(c, odd).wait_recv()
        wide_copy(c).start()

    def pair_one(c, odd):
        pair_copy(c).wait_recv()
        total = own[:, cols(c)] + recv_a[:, cols(c)].astype(f32)
        send_b[:, cols(c)] = total[16:].astype(bf16)
        own[:16, cols(c)] = total[:16]
        start(three_copies(c, odd))

    def three(c, odd):
        for one in three_copies(c, odd):
            one.wait_recv()
        total = own[:16, cols(c)]
        for q in range(3):
            total = total + recv_b[16 * q : 16 * q + 16, cols(c)].astype(f32)
        y[piece(0), cols(c)] = total.astype(bf16)
        start(all_copies(c))

    def wide_one(c, odd):
        for one in all_copies(c):
            one.wait_recv()
        wide_copy(c).start()

    def end(c, odd):
        wide_copy(c).wait_recv()

    stages = [(lag, f, 0, TWO) for lag, f in zip(LAGS_TWO, (pair_two, first, second, back, wide_two, end))]
    stages += [(lag, f, TWO, CHUNKS) for lag, f in zip(LAGS_ONE, (pair_one, three, wide_one, end))]
    stages.sort(key=lambda s: (s[0], -s[2]))

    def steps(lo, hi):
        def two_steps(t, _):
            for odd in (0, 1):
                i = 2 * t + odd
                if lo < CHUNKS:
                    compute(i, odd)
                for lag, stage, begin, stop in stages:
                    c, c_odd = i - lag, (odd + lag) % 2
                    if hi - 1 - lag < begin or lo - lag >= stop:
                        continue
                    if lo - lag >= begin and hi - 1 - lag < stop:
                        stage(c, c_odd)
                        continue

                    @pl.when((c >= begin) & (c < stop))
                    def _(stage=stage, c=c, c_odd=c_odd):
                        stage(c, c_odd)

            return 0

        lax.fori_loop(lo // 2, hi // 2, two_steps, 0)

    last = max(TWO - 1 + LAGS_TWO[-1] if TWO else 0, CHUNKS - 1 + LAGS_ONE[-1] if TWO < CHUNKS else 0) + 1
    steps(0, CHUNKS)
    steps(CHUNKS, last + last % 2)

    def drain(t, _):
        for odd in (0, 1):
            c = 2 * t + odd
            pair_copy(c).wait_send()
            wide_copy(c).wait_send()

            @pl.when(c < TWO)
            def _(c=c, odd=odd):
                for one in (first_copy(c, odd), second_copy(c, odd), *two_copies(c, odd), back_copy(c, odd)):
                    one.wait_send()

            @pl.when(c >= TWO)
            def _(c=c, odd=odd):
                for one in three_copies(c, odd) + all_copies(c):
                    one.wait_send()

        return 0

    lax.fori_loop(0, CHUNKS // 2, drain, 0)


def solution(mesh):
    bf16, f32 = jnp.bfloat16, jnp.float32

    def step(x, w_gate, w_up, w_down):
        dma = pltpu.SemaphoreType.DMA
        return pl.pallas_call(
            kernel,
            out_shape=pltpu.VMEM((ROWS, D), bf16),
            in_specs=[pl.BlockSpec(memory_space=pl.ANY)] * 4,
            out_specs=pl.BlockSpec(memory_space=pltpu.VMEM),
            scratch_shapes=[
                pltpu.VMEM((ROWS, D), bf16),
                pltpu.VMEM((ROWS, H), bf16),
                pltpu.VMEM((ROWS, WIDTH), f32),
                pltpu.VMEM((ROWS, WIDTH), f32),
                pltpu.VMEM((SLOTS, KB, KB), bf16),
                pltpu.VMEM((ROWS, NB), f32),
                pltpu.VMEM((64, D), f32),
                pltpu.VMEM((64, D), bf16),
                pltpu.VMEM((64, D), bf16),
                pltpu.VMEM((48, D), bf16),
                pltpu.VMEM((48, D), bf16),
                dma((8,)),
                dma((SLOTS, 3)),
                dma((8, CHUNKS)),
                dma((8, CHUNKS)),
            ],
            compiler_params=pltpu.CompilerParams(
                collective_id=0, has_side_effects=True, vmem_limit_bytes=60 << 20
            ),
            cost_estimate=pl.CostEstimate(
                flops=6 * ROWS * D * H, bytes_accessed=6 * D * H + 4 * ROWS * D, transcendentals=ROWS * H
            ),
        )(x, w_gate, w_up, w_down)

    return jax.shard_map(
        step,
        mesh=mesh,
        in_specs=(P("dp", None), P(None, "tp"), P(None, "tp"), P("tp", None)),
        out_specs=P("dp", None),
        check_vma=False,
    )
```

time: 188 us -> 113 us (0.60)
  Pallas kernels: 0 us -> 111 us
  matrix products: 108 us -> 0 us
  waiting for transfers between devices: 61 us -> 0 us
  between operations: 13.4 us -> 0.01 us
  local copies, waits for them, and re-layouts: 5.72 us -> 1.67 us
    pallas_call x0 -> x1, Pallas kernels: none -> 111 us  [step(): pl.pallas_call(kernel, out_shape=pltpu.VMEM((ROWS, D), bf16), in_specs=[p...]
    dot_general x3 -> x0, matrix products: 108 us -> none  [the longest x1 36.4 us: step(): jnp.dot(hidden, w_down, preferred_element_type=jnp.float32)]
    psum x1 -> x0, waiting for transfers between devices: 61 us -> none  [step(): return lax.psum(term, 'tp')]
    unnamed x3 -> x1, local copies, waits for them, and re-layouts: 5.72 us -> 1.67 us
  transfers between devices with their start and end apart: 1 -> 0, of which waited for: 1 -> 0; matrix products, arithmetic and copies ran while one was open for 0% -> 0% of each run, Pallas kernels for 0% -> 0%
where the time goes in v6:
time: 113 us
  Pallas kernels  111 us (98%)
  local copies, waits for them, and re-layouts  1.67 us (1%)
    pallas_call x1, Pallas kernels, step(): pl.pallas_call(kernel, out_shape=pltpu.VMEM((ROWS, D), bf16), in_specs=[p...  111 us

profile of v6, /device:TPU:0, one launch (start us, length us, event | category | flops | bytes accessed | tf_op | source)
XLA Modules:
  0.0 112.9 jit_solution(179868483483130694)
XLA Ops:
  0.0 111.2 %shard_map.46 = bf16[128,12288]{1,0:T(8,128)(2,1)S(1)} custom-call(bf16[128,12288]{1,0:T(8,128)(2,1)} %x_hbm.1, bf16[12288,4224]{1,0:T(8,128)(2,1)} %g_hbm.1, bf16[12288,4224]{1,0:T(8,128)(2,1)} %u_hbm.1, bf16[4224,12288]{1,0:T(8,128)(2,1)} %d_hbm.1), custom_call_target="tpu_custom_call" | custom-call | flops 39862665216 | bytes 317718528 | tf_op jit(solution)/shard_map/pallas_call | solution.py:288
  111.2 1.7 %copy.6 = bf16[128,12288]{1,0:T(8,128)(2,1)} copy(bf16[128,12288]{1,0:T(8,128)(2,1)S(1)} %shard_map.46) | data formatting | bytes 6291456

commit v7 on v6

--- a/solution.py
+++ b/solution.py
@@ -14,7 +14,7 @@
 TWO = 20
 LAGS_TWO = (1, 4, 7, 10, 13, 15)
 LAGS_ONE = (1, 5, 9, 11)
-SLOTS = 8
+SLOTS = 4
 WIDTH = 1408
 KS, TILES = D // KB, D // KB * (H // WIDTH)
 

time: 113 us -> 113 us (level)
  no operation moved by 1% of the time
where the time goes in v7:
time: 113 us
  Pallas kernels  111 us (98%)
  local copies, waits for them, and re-layouts  1.67 us (1%)
    pallas_call x1, Pallas kernels, step(): pl.pallas_call(kernel, out_shape=pltpu.VMEM((ROWS, D), bf16), in_specs=[p...  111 us

profile of v7, /device:TPU:0, one launch (start us, length us, event | category | flops | bytes accessed | tf_op | source)
XLA Modules:
  0.0 112.6 jit_solution(15009801521065545362)
XLA Ops:
  0.0 110.9 %shard_map.46 = bf16[128,12288]{1,0:T(8,128)(2,1)S(1)} custom-call(bf16[128,12288]{1,0:T(8,128)(2,1)} %x_hbm.1, bf16[12288,4224]{1,0:T(8,128)(2,1)} %g_hbm.1, bf16[12288,4224]{1,0:T(8,128)(2,1)} %u_hbm.1, bf16[4224,12288]{1,0:T(8,128)(2,1)} %d_hbm.1), custom_call_target="tpu_custom_call" | custom-call | flops 39862665216 | bytes 317718528 | tf_op jit(solution)/shard_map/pallas_call | solution.py:288
  110.9 1.7 %copy.6 = bf16[128,12288]{1,0:T(8,128)(2,1)} copy(bf16[128,12288]{1,0:T(8,128)(2,1)S(1)} %shard_map.46) | data formatting | bytes 6291456

commit v8 on v7

--- a/solution.py
+++ b/solution.py
@@ -11,9 +11,9 @@
 COLS = ((0, 1536), (1536, 1536), (3072, 1152))
 NB = 512
 CHUNKS = D // NB
-TWO = 20
+TWO = 0
 LAGS_TWO = (1, 4, 7, 10, 13, 15)
-LAGS_ONE = (1, 5, 9, 11)
+LAGS_ONE = (1, 4, 7, 9)
 SLOTS = 4
 WIDTH = 1408
 KS, TILES = D // KB, D // KB * (H // WIDTH)
@@ -231,7 +231,7 @@
 
     stages = [(lag, f, 0, TWO) for lag, f in zip(LAGS_TWO, (pair_two, first, second, back, wide_two, end))]
     stages += [(lag, f, TWO, CHUNKS) for lag, f in zip(LAGS_ONE, (pair_one, three, wide_one, end))]
-    stages.sort(key=lambda s: (s[0], -s[2]))
+    stages = sorted((s for s in stages if s[2] < s[3]), key=lambda s: (s[0], -s[2]))
 
     def steps(lo, hi):
         def two_steps(t, _):

time: 113 us -> 113 us (level)
  no operation moved by 1% of the time
where the time goes in v8:
time: 113 us
  Pallas kernels  111 us (98%)
  local copies, waits for them, and re-layouts  1.67 us (1%)
    pallas_call x1, Pallas kernels, step(): pl.pallas_call(kernel, out_shape=pltpu.VMEM((ROWS, D), bf16), in_specs=[p...  111 us

profile of v8, /device:TPU:0, one launch (start us, length us, event | category | flops | bytes accessed | tf_op | source)
XLA Modules:
  0.0 112.7 jit_solution(6454109115393858048)
XLA Ops:
  0.0 111.0 %shard_map.46 = bf16[128,12288]{1,0:T(8,128)(2,1)S(1)} custom-call(bf16[128,12288]{1,0:T(8,128)(2,1)} %x_hbm.1, bf16[12288,4224]{1,0:T(8,128)(2,1)} %g_hbm.1, bf16[12288,4224]{1,0:T(8,128)(2,1)} %u_hbm.1, bf16[4224,12288]{1,0:T(8,128)(2,1)} %d_hbm.1), custom_call_target="tpu_custom_call" | custom-call | flops 39862665216 | bytes 317718528 | tf_op jit(solution)/shard_map/pallas_call | solution.py:288
  111.0 1.7 %copy.6 = bf16[128,12288]{1,0:T(8,128)(2,1)} copy(bf16[128,12288]{1,0:T(8,128)(2,1)S(1)} %shard_map.46) | data formatting | bytes 6291456

commit v9 on v7

--- a/solution.py
+++ b/solution.py
@@ -152,10 +152,9 @@
 
     def compute(c, odd):
         slot = lax.rem(c, SLOTS)
-        for r in range(3):
-            down_copy(c, slot, r).wait()
         total = None
         for r, (at, depth) in enumerate(COLS):
+            down_copy(c, slot, r).wait()
             part = jnp.dot(
                 hidden[:, at : at + depth], ring[slot, :depth, r * NB : (r + 1) * NB], preferred_element_type=f32
             )

time: 113 us -> 112 us (level)
  no operation moved by 1% of the time
where the time goes in v9:
time: 112 us
  Pallas kernels  111 us (99%)
  local copies, waits for them, and re-layouts  1.67 us (1%)
    pallas_call x1, Pallas kernels, step(): pl.pallas_call(kernel, out_shape=pltpu.VMEM((ROWS, D), bf16), in_specs=[p...  111 us

profile of v9, /device:TPU:0, one launch (start us, length us, event | category | flops | bytes accessed | tf_op | source)
XLA Modules:
  0.0 112.3 jit_solution(2641676281469727871)
XLA Ops:
  0.0 110.6 %shard_map.46 = bf16[128,12288]{1,0:T(8,128)(2,1)S(1)} custom-call(bf16[128,12288]{1,0:T(8,128)(2,1)} %x_hbm.1, bf16[12288,4224]{1,0:T(8,128)(2,1)} %g_hbm.1, bf16[12288,4224]{1,0:T(8,128)(2,1)} %u_hbm.1, bf16[4224,12288]{1,0:T(8,128)(2,1)} %d_hbm.1), custom_call_target="tpu_custom_call" | custom-call | flops 39862665216 | bytes 317718528 | tf_op jit(solution)/shard_map/pallas_call | solution.py:287
  110.6 1.7 %copy.6 = bf16[128,12288]{1,0:T(8,128)(2,1)} copy(bf16[128,12288]{1,0:T(8,128)(2,1)S(1)} %shard_map.46) | data formatting | bytes 6291456
